TPU v7x, 32 devices: a whole 2x2x4 slice. The times are simulated.
32 devices in a mesh: rows: 8 (over z, y), cols: 4 (over x, core).
Axes of the slice: x: 2, y: 2, z: 4, core: 2. Of those that a mesh axis runs over, the one named last changes fastest.
Arguments:
- gradients: float32 [32, 128, 4096], P(None, 'rows', 'cols'), may hold values from -6 to 6
- momentum: float32 [32, 128, 4096], P(None, 'rows', 'cols'), may hold values from -6 to 6
- weights: float32 [32, 128, 4096], P(None, 'rows', 'cols'), may hold values from -0.1875 to 0.1875
Outputs:
- new_weights: float32 [32, 128, 4096], P(None, 'rows', 'cols')
- new_momentum: float32 [32, 128, 4096], P(None, 'rows', 'cols')
All inputs are finite; a program needn't handle non-finite values.
Results may differ from a plain program's by a relative error of at most 0.0003.
Values sent between devices are 32-bit elements.
A program may use at most 64 MiB of HBM per device.

v0:
```python
import jax
import jax.numpy as jnp
from jax import lax
from jax.sharding import PartitionSpec as P

ITERS = 4
hold_rate = 0.8
learn_rate = 0.8
decay_rate = 0.1


def mul(a, b):
    return jnp.einsum("mij,mjk->mik", a, b, precision=lax.Precision.HIGHEST)


def local(gradients, momentum, weights):
    new_momentum = hold_rate * momentum + gradients
    whole = lax.all_to_all(new_momentum, "rows", split_axis=0, concat_axis=1, tiled=True)
    gram = jnp.einsum("mik,mjk->mij", whole, whole, precision=lax.Precision.HIGHEST)
    gram = lax.psum(gram, "cols")
    eye = jnp.eye(gram.shape[-1], dtype=jnp.float32)
    total = jnp.sum(gram * eye, axis=(1, 2), keepdims=True)
    scale = lax.rsqrt(total + 1e-06)
    gram = gram * scale * scale
    chain = scale * eye
    for step in range(ITERS):
        factor = 3.4445 * eye - 4.775 * gram + 2.0315 * mul(gram, gram)
        chain = mul(factor, chain)
        if step < ITERS - 1:
            gram = mul(factor, mul(gram, factor))
    iterate = mul(chain, whole)
    back = lax.all_to_all(iterate, "rows", split_axis=1, concat_axis=0, tiled=True)
    new_weights = (1.0 - learn_rate * decay_rate) * weights - learn_rate * back
    return (new_weights, new_momentum)


def solution(mesh):
    placed = (P(None, "rows", "cols"), P(None, "rows", "cols"), P(None, "rows", "cols"))
    return jax.shard_map(
        local,
        mesh=mesh,
        in_specs=placed,
        out_specs=(P(None, "rows", "cols"), P(None, "rows", "cols")),
        check_vma=False,
    )
```

profile of v0, /device:TPU:0, one launch (start us, length us, event | category | flops | bytes accessed | tf_op | source)
XLA Modules:
  0.0 175.1 jit_solution(10635801916381420988)
XLA Ops:
  7.2 0.0 all-reduce.2.cloned.1.call-start
  7.2 2.7 %multiply_add_fusion = f32[32,16,1024]{2,1,0:T(8,128)S(1)} fusion(f32[32,16,1024]{2,1,0:T(8,128)} %param.3, f32[32,16,1024]{2,1,0:T(8,128)} %param.4), kind=kLoop, calls=%fused_computation.1 | loop fusion | flops 1048576 | bytes 6291456 | tf_op jit(solution)/shard_map/add | solution.py:17
  9.9 0.0 copy-start
  9.9 55.3 %all_to_all.27 = f32[32,16,1024]{2,1,0:T(8,128)S(1)} all-to-all(f32[32,16,1024]{2,1,0:T(8,128)S(1)} %multiply_add_fusion), channel_id=1, replica_groups=mesh['rows'=8,'cols'=4] {'rows'}, dimensions={0} | all-to-all | bytes 4194304 | tf_op jit(solution)/shard_map/all_to_all | solution.py:18
  65.2 0.0 copy-done
  65.2 0.1 copy.7
  65.4 2.8 %fusion.13 = f32[4,128,128]{2,1,0:T(8,128)} fusion(f32[4,128,1024]{2,1,0:T(8,128)S(1)} %bitcast.37), kind=kOutput, calls=%fused_computation.24 | convolution fusion | flops 805306368 | bytes 2359296 | tf_op jit(solution)/shard_map/mik,mjk->mij/dot_general | solution.py:19
  68.1 0.0 all-reduce.2.cloned.1.call-update
  68.2 31.4 %all-reduce.2.cloned.1.call-done = f32[4,128,128]{2,1,0:T(8,128)} async-done(((f32[4,128,128]{2,1,0:T(8,128)}), f32[4,128,128]{2,1,0:T(8,128)}) %all-reduce.2.cloned.1.call-update) | async-done | bytes 262160 | tf_op jit(solution)/shard_map/psum | solution.py:20
  99.6 1.1 multiply_reduce_fusion
  100.7 1.6 fusion.3
  102.3 0.4 fusion.4
  102.7 1.4 fusion.6
  104.1 0.4 fusion.14
  104.5 0.4 fusion.2
  104.9 0.4 fusion.15
  105.3 0.4 fusion.19
  105.7 0.4 fusion.16
  106.1 0.4 fusion.1
  106.5 0.4 fusion.17
  106.9 0.4 fusion.20
  107.3 0.4 fusion.18
  107.7 0.4 fusion
  108.1 0.4 fusion.21
  108.5 1.9 %fusion.22 = f32[4,128,1024]{2,1,0:T(8,128)S(1)} fusion(f32[4,128,128]{2,1,0:T(8,128)S(1)} %fusion.21, f32[4,128,1024]{2,1,0:T(8,128)S(1)} %bitcast.38), kind=kOutput, calls=%fused_computation.33 | convolution fusion | flops 805306368 | bytes 4456448 | tf_op jit(solution)/shard_map/mij,mjk->mik/dot_general | solution.py:13
  110.4 1.4 copy.8
  111.8 52.5 %all_to_all.28 = f32[4,128,1024]{2,0,1:T(4,128)S(1)} all-to-all(f32[4,128,1024]{2,0,1:T(4,128)S(1)} %copy.8), channel_id=1, replica_groups=mesh['rows'=8,'cols'=4] {'rows'}, dimensions={1} | all-to-all | bytes 4194304 | tf_op jit(solution)/shard_map/all_to_all | solution.py:32
  164.3 0.6 broadcast_multiply_fusion
  164.9 0.0 copy-start.1
  164.9 1.2 copy.9
  166.1 0.4 copy-done.1
  166.5 1.8 %bitcast_subtract_fusion = f32[32,16,1024]{2,1,0:T(8,128)} fusion(f32[8,4,16,1024]{3,2,1,0:T(8,128)S(1)} %copy.9, f32[32,16,1024]{2,1,0:T(8,128)S(1)} %copy-done.1), kind=kLoop, calls=%fused_computation | loop fusion | flops 1048576 | bytes 6291456 | tf_op jit(solution)/shard_map/sub | solution.py:33
  (3 shorter events, 0.0 us)
Async XLA Ops:
  7.2 92.4 %all-reduce.2.cloned.1.call-start = ((), (), s32[]{:S(2)}) async-start(), calls=%async_computation.2 | async-start | bytes 524288 | tf_op jit(solution)/shard_map/psum | solution.py:20
  9.9 55.4 %copy-start = (f32[32,16,1024]{2,1,0:T(8,128)}, f32[32,16,1024]{2,1,0:T(8,128)S(1)}, u32[]{:S(2)}) copy-start(f32[32,16,1024]{2,1,0:T(8,128)S(1)} %multiply_add_fusion) | copy-start | bytes 6291460
  164.9 1.6 copy-start.1
Sparse Core Ops, SparseCore 0:
  68.3 31.2 all-reduce.1
where the time goes:
time: 175 us
  blocking collectives  108 us (62%)
  waiting for transfers between devices  31.4 us (18%)
  between operations  14.2 us (8%)
  matrix products  12.4 us (7%)
  other arithmetic  6.1 us (3%)
  local copies, waits for them, and re-layouts  3.07 us (2%)
    all_to_all x1, blocking collectives, local(): lax.all_to_all(new_momentum, 'rows', split_axis=0, concat_axis=1, tiled=T...  55.3 us
    all_to_all x1, blocking collectives, local(): lax.all_to_all(iterate, 'rows', split_axis=1, concat_axis=0, tiled=True)  52.5 us
    psum x1, waiting for transfers between devices, local(): gram = lax.psum(gram, 'cols')  31.4 us
    dot_general x15, matrix products, mul(): return jnp.einsum('mij,mjk->mik', a, b, precision=lax.Precision.HIGHEST)  9.64 us
  transfers between devices with their start and end apart: 1, of which 1 were waited for; matrix products, arithmetic and copies ran while one was open for 0% of the time, Pallas kernels for 0%

commit v1 on v0

--- a/solution.py
+++ b/solution.py
@@ -15,7 +15,12 @@
 
 def local(gradients, momentum, weights):
     new_momentum = hold_rate * momentum + gradients
-    whole = lax.all_to_all(new_momentum, "rows", split_axis=0, concat_axis=1, tiled=True)
+    whole = jnp.concatenate(
+        lax.all_to_all(
+            jnp.stack(jnp.split(new_momentum, lax.axis_size("rows"), axis=0)), "rows", 0, 0
+        ),
+        axis=1,
+    )
     gram = jnp.einsum("mik,mjk->mij", whole, whole, precision=lax.Precision.HIGHEST)
     gram = lax.psum(gram, "cols")
     eye = jnp.eye(gram.shape[-1], dtype=jnp.float32)

time: 175 us -> 177 us (1.011)
  no operation moved by 1% of the time
where the time goes in v1:
time: 177 us
  blocking collectives  108 us (61%)
  waiting for transfers between devices  31.4 us (18%)
  between operations  14.3 us (8%)
  matrix products  12.4 us (7%)
  other arithmetic  6.28 us (4%)
  local copies, waits for them, and re-layouts  4.32 us (2%)
    all_to_all x1, blocking collectives, local(): lax.all_to_all(jnp.stack(jnp.split(new_momentum, lax.axis_size('rows'), a...  55.3 us
    all_to_all x1, blocking collectives, local(): lax.all_to_all(iterate, 'rows', split_axis=1, concat_axis=0, tiled=True)  52.5 us
    psum x1, waiting for transfers between devices, local(): gram = lax.psum(gram, 'cols')  31.4 us
    dot_general x15, matrix products, mul(): return jnp.einsum('mij,mjk->mik', a, b, precision=lax.Precision.HIGHEST)  9.65 us
  transfers between devices with their start and end apart: 1, of which 1 were waited for; matrix products, arithmetic and copies ran while one was open for 0% of the time, Pallas kernels for 0%

profile of v1, /device:TPU:0, one launch (start us, length us, event | category | flops | bytes accessed | tf_op | source)
XLA Modules:
  0.0 176.5 jit_solution(13294960395621938709)
XLA Ops:
  7.2 0.0 all-reduce.2.cloned.1.call-start
  7.2 2.8 %multiply_add_fusion = f32[32,16,1024]{2,1,0:T(8,128)S(1)} fusion(f32[32,16,1024]{2,1,0:T(8,128)} %param.3, f32[32,16,1024]{2,1,0:T(8,128)} %param.4), kind=kLoop, calls=%fused_computation.1 | loop fusion | flops 1048576 | bytes 6291456 | tf_op jit(solution)/shard_map/add | solution.py:17
  10.0 0.0 copy-start
  10.3 1.1 copy-done
  11.4 55.3 %all_to_all.14 = f32[8,4,16,1024]{3,2,1,0:T(8,128)S(1)} all-to-all(f32[8,4,16,1024]{3,2,1,0:T(8,128)S(1)} %fusion.4), channel_id=1, replica_groups=mesh['rows'=8,'cols'=4] {'rows'}, dimensions={0} | all-to-all | bytes 4194304 | tf_op jit(solution)/shard_map/all_to_all | solution.py:19
  66.7 0.1 copy.7
  66.8 2.8 %fusion.21 = f32[4,128,128]{2,1,0:T(8,128)} fusion(f32[4,128,1024]{2,1,0:T(8,128)S(1)} %bitcast.67), kind=kOutput, calls=%fused_computation.40 | convolution fusion | flops 805306368 | bytes 2359296 | tf_op jit(solution)/shard_map/mik,mjk->mij/dot_general | solution.py:24
  69.6 0.0 all-reduce.2.cloned.1.call-update
  69.7 31.4 %all-reduce.2.cloned.1.call-done = f32[4,128,128]{2,1,0:T(8,128)} async-done(((f32[4,128,128]{2,1,0:T(8,128)}), f32[4,128,128]{2,1,0:T(8,128)}) %all-reduce.2.cloned.1.call-update) | async-done | bytes 262160 | tf_op jit(solution)/shard_map/psum | solution.py:25
  101.1 1.1 multiply_reduce_fusion
  102.1 1.6 fusion.3
  103.8 0.4 fusion.12
  104.2 1.4 fusion.14
  105.6 0.4 fusion.22
  106.0 0.4 fusion.2
  106.4 0.4 fusion.23
  106.8 0.4 fusion.27
  107.2 0.4 fusion.24
  107.6 0.4 fusion.1
  108.0 0.4 fusion.25
  108.4 0.4 fusion.28
  108.8 0.4 fusion.26
  109.2 0.4 fusion
  109.6 0.4 fusion.29
  110.0 1.9 %fusion.30 = f32[4,128,1024]{2,1,0:T(8,128)S(1)} fusion(f32[4,128,128]{2,1,0:T(8,128)S(1)} %fusion.29, f32[4,128,1024]{2,1,0:T(8,128)S(1)} %bitcast.68), kind=kOutput, calls=%fused_computation.49 | convolution fusion | flops 805306368 | bytes 4456448 | tf_op jit(solution)/shard_map/mij,mjk->mik/dot_general | solution.py:13
  111.9 1.4 copy.8
  113.3 52.5 %all_to_all.15 = f32[4,128,1024]{2,0,1:T(4,128)S(1)} all-to-all(f32[4,128,1024]{2,0,1:T(4,128)S(1)} %copy.8), channel_id=1, replica_groups=mesh['rows'=8,'cols'=4] {'rows'}, dimensions={1} | all-to-all | bytes 4194304 | tf_op jit(solution)/shard_map/all_to_all | solution.py:37
  165.7 0.6 broadcast_multiply_fusion
  166.3 0.0 copy-start.1
  166.4 1.2 copy.9
  167.6 0.4 copy-done.1
  167.9 1.8 bitcast_subtract_fusion
  (11 shorter events, 0.2 us)
Async XLA Ops:
  7.2 93.9 %all-reduce.2.cloned.1.call-start = ((), (), s32[]{:S(2)}) async-start(), calls=%async_computation.2 | async-start | bytes 524288 | tf_op jit(solution)/shard_map/psum | solution.py:25
  10.0 1.3 copy-start
  166.3 1.6 copy-start.1
Sparse Core Ops, SparseCore 0:
  69.7 31.2 all-reduce.1

commit v2 on v0

--- a/solution.py
+++ b/solution.py
@@ -17,7 +17,7 @@
     new_momentum = hold_rate * momentum + gradients
     whole = lax.all_to_all(new_momentum, "rows", split_axis=0, concat_axis=1, tiled=True)
     gram = jnp.einsum("mik,mjk->mij", whole, whole, precision=lax.Precision.HIGHEST)
-    gram = lax.psum(gram, "cols")
+    gram = jnp.sum(lax.all_gather(gram, "cols"), axis=0)
     eye = jnp.eye(gram.shape[-1], dtype=jnp.float32)
     total = jnp.sum(gram * eye, axis=(1, 2), keepdims=True)
     scale = lax.rsqrt(total + 1e-06)

time: 175 us -> 160 us (0.914)
  waiting for transfers between devices: 31.4 us -> 15.8 us
  matrix products: 12.4 us -> 10.3 us
    psum x1 -> x0, waiting for transfers between devices: 31.4 us -> none  [local(): gram = lax.psum(gram, 'cols')]
    all_gather x0 -> x1, waiting for transfers between devices: none -> 15.8 us  [local(): gram = jnp.sum(lax.all_gather(gram, 'cols'), axis=0)]
    dot_general x15, matrix products: 9.64 us -> 7.57 us  [mul(): return jnp.einsum('mij,mjk->mik', a, b, precision=lax.Precision.HIGHEST)]
where the time goes in v2:
time: 160 us; the launch traced here: 159 us
  blocking collectives  109 us (68%)
  waiting for transfers between devices  15.8 us (10%)
  between operations  14.2 us (9%)
  matrix products  10.3 us (6%)
  other arithmetic  6.56 us (4%)
  local copies, waits for them, and re-layouts  3.17 us (2%)
    all_to_all x1, blocking collectives, local(): lax.all_to_all(new_momentum, 'rows', split_axis=0, concat_axis=1, tiled=T...  55.3 us
    all_to_all x1, blocking collectives, local(): lax.all_to_all(iterate, 'rows', split_axis=1, concat_axis=0, tiled=True)  53.9 us
    all_gather x1, waiting for transfers between devices, local(): gram = jnp.sum(lax.all_gather(gram, 'cols'), axis=0)  15.8 us
    dot_general x15, matrix products, mul(): return jnp.einsum('mij,mjk->mik', a, b, precision=lax.Precision.HIGHEST)  7.57 us
  transfers between devices with their start and end apart: 1, of which 1 were waited for; matrix products, arithmetic and copies ran while one was open for 0% of the time, Pallas kernels for 0%

profile of v2, /device:TPU:0, one launch (start us, length us, event | category | flops | bytes accessed | tf_op | source)
XLA Modules:
  0.0 159.4 jit_solution(14867783212618348793)
XLA Ops:
  7.2 0.0 all-gather.3.cloned.1.call-start
  7.2 2.7 %multiply_add_fusion = f32[32,16,1024]{2,1,0:T(8,128)S(1)} fusion(f32[32,16,1024]{2,1,0:T(8,128)} %param.3, f32[32,16,1024]{2,1,0:T(8,128)} %param.4), kind=kLoop, calls=%fused_computation.1 | loop fusion | flops 1048576 | bytes 6291456 | tf_op jit(solution)/shard_map/add | solution.py:17
  9.9 0.0 copy-start
  9.9 55.3 %all_to_all.27 = f32[32,16,1024]{2,1,0:T(8,128)S(1)} all-to-all(f32[32,16,1024]{2,1,0:T(8,128)S(1)} %multiply_add_fusion), channel_id=1, replica_groups=mesh['rows'=8,'cols'=4] {'rows'}, dimensions={0} | all-to-all | bytes 4194304 | tf_op jit(solution)/shard_map/all_to_all | solution.py:18
  65.2 0.0 copy-done
  65.2 0.2 copy.7
  65.5 2.8 %fusion.13 = f32[4,128,128]{2,1,0:T(8,128)} fusion(f32[4,128,1024]{2,1,0:T(8,128)S(1)} %bitcast.38), kind=kOutput, calls=%fused_computation.24 | convolution fusion | flops 805306368 | bytes 2359296 | tf_op jit(solution)/shard_map/mik,mjk->mij/dot_general | solution.py:19
  68.2 0.0 all-gather.3.cloned.1.call-update
  68.3 15.8 %all-gather.3.cloned.1.call-done = f32[16,128,128]{2,1,0:T(8,128)} async-done(((f32[4,128,128]{2,1,0:T(8,128)}), f32[16,128,128]{2,1,0:T(8,128)}) %all-gather.3.cloned.1.call-update) | async-done | bytes 1048592 | tf_op jit(solution)/shard_map/all_gather | solution.py:20
  84.1 1.3 reduce_sum.18
  85.4 0.1 multiply_reduce_fusion
  85.6 0.5 fusion.3
  86.1 0.4 fusion.6
  86.5 0.4 fusion.4
  87.0 0.4 fusion.14
  87.4 0.4 fusion.2
  87.7 0.4 fusion.15
  88.1 0.4 fusion.19
  88.5 0.4 fusion.16
  88.9 0.4 fusion.1
  89.3 0.4 fusion.17
  89.7 0.4 fusion.20
  90.1 0.4 fusion.18
  90.5 0.4 fusion
  90.9 0.4 fusion.21
  91.3 1.9 %fusion.22 = f32[4,128,1024]{2,1,0:T(8,128)S(1)} fusion(f32[4,128,128]{2,1,0:T(8,128)S(1)} %fusion.21, f32[4,128,1024]{2,1,0:T(8,128)S(1)} %bitcast.39), kind=kOutput, calls=%fused_computation.33 | convolution fusion | flops 805306368 | bytes 4456448 | tf_op jit(solution)/shard_map/mij,mjk->mik/dot_general | solution.py:13
  93.2 1.4 copy.8
  94.6 53.9 %all_to_all.28 = f32[4,128,1024]{2,0,1:T(4,128)S(1)} all-to-all(f32[4,128,1024]{2,0,1:T(4,128)S(1)} %copy.8), channel_id=1, replica_groups=mesh['rows'=8,'cols'=4] {'rows'}, dimensions={1} | all-to-all | bytes 4194304 | tf_op jit(solution)/shard_map/all_to_all | solution.py:32
  148.5 0.7 broadcast_multiply_fusion
  149.2 0.0 copy-start.1
  149.2 1.2 copy.9
  150.4 0.4 copy-done.1
  150.8 1.8 %bitcast_subtract_fusion = f32[32,16,1024]{2,1,0:T(8,128)} fusion(f32[8,4,16,1024]{3,2,1,0:T(8,128)S(1)} %copy.9, f32[32,16,1024]{2,1,0:T(8,128)S(1)} %copy-done.1), kind=kLoop, calls=%fused_computation | loop fusion | flops 1048576 | bytes 6291456 | tf_op jit(solution)/shard_map/sub | solution.py:33
  (3 shorter events, 0.0 us)
Async XLA Ops:
  7.2 76.9 %all-gather.3.cloned.1.call-start = ((), (), s32[]{:S(2)}) async-start(), calls=%async_computation.2 | async-start | bytes 1310720 | tf_op jit(solution)/shard_map/all_gather | solution.py:20
  9.9 55.4 %copy-start = (f32[32,16,1024]{2,1,0:T(8,128)}, f32[32,16,1024]{2,1,0:T(8,128)S(1)}, u32[]{:S(2)}) copy-start(f32[32,16,1024]{2,1,0:T(8,128)S(1)} %multiply_add_fusion) | copy-start | bytes 6291460
  149.2 1.6 %copy-start.1 = (f32[32,16,1024]{2,1,0:T(8,128)S(1)}, f32[32,16,1024]{2,1,0:T(8,128)}, u32[]{:S(2)}) copy-start(f32[32,16,1024]{2,1,0:T(8,128)} %param.5) | copy-start | bytes 6291460
Sparse Core Ops, SparseCore 0:
  68.4 15.6 all-gather.2
